TPU v7x, 32 devices: a whole 2x2x4 slice. The times are simulated.
32 devices in a mesh: group: 2 (over y), tp: 16 (over z, x, core).
Axes of the slice: x: 2, y: 2, z: 4, core: 2. Of those that a mesh axis runs over, the one named last changes fastest.
Arguments:
- queries: bfloat16 [2, 8, 2, 8192], P('group', None, None, 'tp'), may hold values from -24 to 24
- new_keys: bfloat16 [2, 8, 2, 1024], P('group', None, None, 'tp'), may hold values from -16 to 16
- new_values: bfloat16 [2, 8, 2, 1024], P('group', None, None, 'tp'), may hold values from -24 to 24
- key_pages: bfloat16 [2, 1024, 16, 1024], P('group', 'tp'), may hold values from -16 to 16
- value_pages: bfloat16 [2, 1024, 16, 1024], P('group', 'tp'), may hold values from -24 to 24
- page_owner: int32 [2, 1024], P('group', 'tp'), may hold values from 0 to 8, as said below
- page_fill: int32 [2, 1024], P('group', 'tp'), may hold values from 0 to 16, as said below
- target_slot: int32 [2, 8], P('group'), may hold values from 0 to 8, as said below
- out_weight: bfloat16 [8192, 8192], P(None, 'tp'), may hold values from -0.0625 to 0.0625
Outputs:
- projected: bfloat16 [2, 8, 2, 8192], P('group', None, None, 'tp')
Inputs may be any that keep to these rules, and one draw needn't show every extreme that they name: `page_owner`: the owning request slot, or 8 for a free page. Of each pair of groups g and g XOR (1) one is loaded (no free pages) and the other light; group 0 is light, and so is group 2 - 1 when 2 > 2. One device holds at most 16 pages of moving requests, and some device of every loaded group holds exactly 16. `page_fill`: 1 to 16 for a used page, 0 for a free one. `target_slot`: 8 for a request that stays. Every group has exactly one moving request; their slots in the partner group are distinct and own no pages there.
All inputs are finite; a program needn't handle non-finite values.
Results may differ from a plain program's by a relative error of at most 0.0065.
Values may be sent and summed in bfloat16 or wider, within the bound.
No kernel may reach another device: no remote copies, remote signals or barrier semaphores. Data moves between devices by JAX's collectives and lax.ppermute only.
A program may use at most 64 MiB of HBM per device.

v0:
```python
import math
import jax
import jax.numpy as jnp
from jax import lax
from jax.sharding import PartitionSpec as P

HEADS = 64
KVH = 8
HD = 128
PAGE = 16
MOVE = 1
neg_big = -1e30


def swapped(value, axis, distance):
    return lax.ppermute(value, axis, [(i, i ^ 1 << distance) for i in range(lax.axis_size(axis))])


def combined_all(part, axis, combine):
    gathered = jax.tree.map(lambda a: lax.all_gather(a, axis), part)

    def take(source):
        return jax.tree.map(lambda a: lax.dynamic_index_in_dim(a, source, 0, False), gathered)

    return lax.fori_loop(
        1, lax.axis_size(axis), lambda source, state: combine(state, take(source)), take(0)
    )


def merge_states(first, second):
    largest = jnp.maximum(first[0], second[0])
    scale_first = jnp.exp(first[0] - largest)
    scale_second = jnp.exp(second[0] - largest)
    return (
        largest,
        first[1] * scale_first + second[1] * scale_second,
        first[2] * scale_first[..., None] + second[2] * scale_second[..., None],
    )


def page_states(query_rows, key_block, value_block, owner_rows, fill_counts, row_count):
    page_count = key_block.shape[0]
    step_count = query_rows.shape[1]
    group_size = HEADS // KVH
    scale_factor = 1.0 / math.sqrt(HD)
    clipped = jnp.clip(owner_rows, 0, row_count - 1)
    query_page = jnp.take(query_rows, clipped, axis=0).reshape(
        page_count, step_count, KVH, group_size, HD
    )
    key_page = key_block.reshape(page_count, PAGE, KVH, HD)
    value_page = value_block.reshape(page_count, PAGE, KVH, HD)
    scores = (
        jnp.einsum("psgjd,ptgd->psgjt", query_page, key_page, preferred_element_type=jnp.float32)
        * scale_factor
    )
    live_token = (owner_rows < row_count)[:, None] & (
        lax.broadcasted_iota(jnp.int32, (page_count, PAGE), 1) < fill_counts[:, None]
    )
    token_mask = live_token[:, None, None, None, :]
    scores = jnp.where(token_mask, scores, neg_big)
    page_top = jnp.max(scores, axis=4).reshape(page_count, step_count * HEADS)
    member = owner_rows[None, :] == lax.broadcasted_iota(jnp.int32, (row_count, page_count), 0)
    row_top = jnp.max(jnp.where(member[:, :, None], page_top[None], neg_big), axis=1)
    top_page = jnp.take(row_top, clipped, axis=0).reshape(
        page_count, step_count, KVH, group_size, 1
    )
    weights = jnp.where(token_mask, jnp.exp(scores - top_page), 0.0).astype(jnp.bfloat16)
    weighted = jnp.einsum(
        "psgjt,ptgd->psgjd", weights, value_page, preferred_element_type=jnp.float32
    ).reshape(page_count, step_count * HEADS * HD)
    weight_sum = jnp.sum(weights.astype(jnp.float32), axis=4).reshape(
        page_count, step_count * HEADS
    )
    onehot = member.astype(jnp.float32)
    row_sum = jnp.dot(onehot, weight_sum, precision=lax.Precision.HIGHEST)
    row_acc = jnp.dot(onehot, weighted, precision=lax.Precision.HIGHEST)
    return (
        row_top.reshape(row_count, step_count, HEADS),
        row_sum.reshape(row_count, step_count, HEADS),
        row_acc.reshape(row_count, step_count, HEADS, HD),
    )


def new_token_states(query_heads, key_rows, value_rows, head_kv):
    row_count = key_rows.shape[0]
    step_count = key_rows.shape[1]
    scale_factor = 1.0 / math.sqrt(HD)
    key_heads = jnp.take(key_rows.reshape(row_count, step_count, KVH, HD), head_kv, axis=2)
    value_heads = jnp.take(
        value_rows.reshape(row_count, step_count, KVH, HD), head_kv, axis=2
    ).astype(jnp.float32)
    scores = (
        jnp.einsum("rshd,ruhd->rshu", query_heads, key_heads, preferred_element_type=jnp.float32)
        * scale_factor
    )
    causal = (
        lax.broadcasted_iota(jnp.int32, (step_count, step_count), 1)
        <= lax.broadcasted_iota(jnp.int32, (step_count, step_count), 0)
    )[None, :, None, :]
    scores = jnp.where(causal, scores, neg_big)
    largest = jnp.max(scores, axis=3)
    weights = jnp.where(causal, jnp.exp(scores - largest[..., None]), 0.0)
    return (
        largest,
        jnp.sum(weights, axis=3),
        jnp.einsum("rshu,ruhd->rshd", weights, value_heads, precision=lax.Precision.HIGHEST),
    )


def per_device(
    queries,
    new_keys,
    new_values,
    key_pages,
    value_pages,
    page_owner,
    page_fill,
    target_slot,
    out_weight,
):
    row_count = queries.shape[1]
    step_count = queries.shape[2]
    partner_bit = lax.axis_size("group").bit_length() - 2
    query_rows, key_rows, value_rows = (
        lax.all_gather(queries[0], "tp", axis=2, tiled=True),
        lax.all_gather(new_keys[0], "tp", axis=2, tiled=True),
        lax.all_gather(new_values[0], "tp", axis=2, tiled=True),
    )
    owners = page_owner[0]
    fill_counts = page_fill[0]
    slot_targets = target_slot[0]
    clipped = jnp.clip(owners, 0, row_count - 1)
    page_target = jnp.take(slot_targets, clipped)
    occupied = owners < row_count
    moving = occupied & (page_target < row_count)
    partner_targets = swapped(slot_targets, "group", partner_bit)
    slot_ids = lax.broadcasted_iota(jnp.int32, (row_count,), 0)
    mover_ids = lax.broadcasted_iota(jnp.int32, (MOVE, row_count), 0)
    their_moving = partner_targets < row_count
    their_rank = jnp.cumsum(their_moving.astype(jnp.int32)) - 1
    their_pick = their_moving[None, :] & (their_rank[None, :] == mover_ids)
    pick_rows = jnp.sum(their_pick.astype(jnp.int32) * partner_targets[None, :], axis=1)
    pick_valid = jnp.any(their_pick, axis=1)
    send_pick = pick_valid[:, None] & (pick_rows[:, None] == slot_ids[None, :])
    sent_queries = jnp.einsum(
        "mr,rsd->msd",
        send_pick.astype(jnp.bfloat16),
        query_rows,
        preferred_element_type=jnp.float32,
    ).astype(jnp.bfloat16)
    arrived_queries = swapped(sent_queries, "group", partner_bit)
    own_moving = slot_targets < row_count
    own_rank = jnp.cumsum(own_moving.astype(jnp.int32)) - 1
    page_rank = jnp.take(own_rank, clipped)
    local_rows = jnp.where(
        occupied, jnp.where(moving, row_count + page_rank, owners), row_count + MOVE
    )
    joined = page_states(
        jnp.concatenate([query_rows, arrived_queries], axis=0),
        key_pages[0],
        value_pages[0],
        local_rows,
        fill_counts,
        row_count + MOVE,
    )
    own_part = tuple((member_array[:row_count] for member_array in joined))
    theirs = tuple((member_array[row_count:] for member_array in joined))
    returned = swapped((theirs[0], theirs[1], theirs[2]), "group", partner_bit)
    placement_table = send_pick.astype(jnp.float32)
    placed_any = jnp.any(send_pick, axis=0)
    placed_max = jnp.where(
        placed_any[:, None, None],
        jnp.einsum("mr,msh->rsh", placement_table, returned[0], precision=lax.Precision.HIGHEST),
        neg_big,
    )
    placed_sum = jnp.einsum(
        "mr,msh->rsh", placement_table, returned[1], precision=lax.Precision.HIGHEST
    )
    placed_acc = jnp.einsum(
        "mr,mshd->rshd", placement_table, returned[2], precision=lax.Precision.HIGHEST
    )
    states = merge_states(own_part, (placed_max, placed_sum, placed_acc))
    head_kv_all = lax.broadcasted_iota(jnp.int32, (HEADS,), 0) // (HEADS // KVH)
    query_heads = query_rows.reshape(row_count, step_count, HEADS, HD)
    combined = combined_all((states[0], states[1], states[2]), "tp", merge_states)
    new_terms = new_token_states(query_heads, key_rows, value_rows, head_kv_all)
    finished = merge_states(combined, new_terms)
    attention = (
        (finished[2] / finished[1][..., None])
        .astype(jnp.bfloat16)
        .reshape(row_count * step_count, HEADS * HD)
    )
    projected = jnp.dot(attention, out_weight, preferred_element_type=jnp.float32).astype(
        jnp.bfloat16
    )
    return projected.reshape(1, row_count, step_count, out_weight.shape[1])


def solution(mesh):
    placed = (
        P("group", None, None, "tp"),
        P("group", None, None, "tp"),
        P("group", None, None, "tp"),
        P("group", "tp", None, None),
        P("group", "tp", None, None),
        P("group", "tp"),
        P("group", "tp"),
        P("group", None),
        P(None, "tp"),
    )
    return jax.shard_map(
        per_device,
        mesh=mesh,
        in_specs=placed,
        out_specs=P("group", None, None, "tp"),
        check_vma=False,
    )
```

profile of v0, /device:TPU:0, one launch (start us, length us, event | category | flops | bytes accessed | tf_op | source)
XLA Modules:
  0.0 223.7 jit_solution(14644763378011074717)
XLA Ops:
  6.5 3.0 %collective-permute-start = (s32[8]{0:T(128)}, s32[8]{0:T(128)S(1)}, u32[]{:S(2)}, u32[]{:S(2)}) collective-permute-start(s32[8]{0:T(128)} %bitcast.168), channel_id=1, source_target_pairs={{0,16},{16,0},{1,17},{17,1},{2,18},{18,2},{3,19},{19,3},{4,20},{20... | collective-permute-start | bytes 104 | tf_op jit(solution)/shard_map/ppermute | solution.py:16
  9.5 0.7 fusion.42
  10.2 1.6 fusion.52
  12.0 0.7 fusion.53
  12.7 10.6 %broadcast_compare_fusion = (pred[64]{0:T(512)(128)(4,1)S(1)}, s32[64]{0:T(128)S(1)}) fusion(s32[]{:T(128)} %bitcast.22, s32[]{:T(128)} %bitcast.21, s32[]{:T(128)} %bitcast.20, s32[]{:T(128)} %bitcast.19, s32[]{:T(128)} %bitcast.18, s32[]{:T(128)} %bitcast.17, s32[]{:T(128)} %bitcast.16, s32[]{:T(128)} %bitcast.15, s32[]{:T(128)} %bitcast.12, s32[]{:T(128)} %bitcast.11, ...), kind=kLoop, calls=%fused_computation.120 | loop fusion | flops 2368 | bytes 640 | tf_op jit(solution)/shard_map/lt | solution.py:56
  23.4 22.6 %all-gather = bf16[1,8,2,8192]{3,2,1,0:T(2,128)(2,1)S(1)} all-gather(bf16[1,8,2,512]{3,2,1,0:T(2,128)(2,1)} %param.15), channel_id=2, replica_groups=mesh['group'=2,'tp'=16] {'tp'}, dimensions={3}, use_global_device_ids=true | all-gather | bytes 278528 | tf_op jit(solution)/shard_map/all_gather | solution.py:125
  45.9 2.4 %copy.149 = bf16[128,8,8,128]{3,2,1,0:T(8,128)(2,1)S(1)} copy(bf16[128,8,8,128]{3,1,2,0:T(8,128)(2,1)} %bitcast.155) | data formatting | bytes 4194304
  48.3 1.5 bitcast_bitcast_fusion.1
  49.8 0.6 copy.150
  50.4 1.5 bitcast_bitcast_fusion
  52.2 0.7 select_reduce_fusion.1
  52.9 0.6 fusion.46
  53.6 1.3 compare_and_fusion.2
  54.9 0.4 fusion.22
  55.4 0.6 collective-permute-start.1
  55.9 1.3 fusion.43
  57.3 2.1 collective-permute-done.1
  59.3 0.4 pad_maximum_fusion
  59.7 6.1 %gather_fusion = bf16[64,2,8192]{2,1,0:T(2,128)(2,1)S(1)} fusion(bf16[9,2,8192]{2,1,0:T(2,128)(2,1)S(1)} %pad_maximum_fusion, s32[1024]{0:T(1024)S(1)} %pad_clamp_fusion.1), kind=kCustom, calls=%fused_computation.2 | custom fusion | bytes 4194560 | tf_op jit(solution)/shard_map/jit(_take)/gather | solution.py:47
  65.8 2.9 %gather.19 = bf16[64,2,8,8,128]{4,3,2,1,0:T(8,128)(2,1)} reshape(bf16[64,2,8192]{2,1,0:T(2,128)(2,1)S(1)} %gather_fusion) | data formatting | bytes 4194304 | tf_op jit(solution)/shard_map/jit(_take)/gather | solution.py:47
  68.7 5.8 %bitcast_reduce_fusion = (f32[64,2,8,8]{3,1,2,0:T(2,128)S(1)}, f32[64,8,2,8,16]{4,3,2,1,0:T(8,128)}) fusion(pred[64,16]{1,0:T(8,128)(4,1)S(1)} %fusion.29, bf16[64,16,8,128,1]{3,2,1,0,4:T(8,128)(2,1)} %bitcast_bitcast_fusion.1, bf16[64,2,8,8,128]{4,3,2,1,0:T(8,128)(2,1)} %gather.19, pred[64]{0:T(512)(128)(4,1)S(1)} %get-tuple-element.215), kind=kOutput, calls=%fused_computation.16 | convolution fusion | flops 34988032 | bytes 4752448 | tf_op jit(solution)/shard_map/psgjd,ptgd->psgjt/dot_general | solution.py:53
  75.1 0.6 gather_fusion.1
  75.7 0.6 collective-permute-start.2
  76.4 0.4 copy.112
  76.8 4.9 %convert_reduce_fusion = f32[64,2,8,8]{3,1,2,0:T(2,128)S(1)} fusion(f32[64,2,8,8]{3,1,2,0:T(2,128)S(1)} %copy.112, f32[64,8,2,8,16]{4,3,2,1,0:T(8,128)} %get-tuple-element.238, pred[64,16]{1,0:T(8,128)(4,1)S(1)} %fusion.29), kind=kLoop, calls=%fused_computation.20 | loop fusion | flops 909312 | bytes 590848 | tf_op jit(solution)/shard_map/reduce_sum | solution.py:71
  81.7 0.3 copy.113
  82.3 1.5 collective-permute-start.3
  83.8 4.2 %convolution_bitcast_fusion = f32[64,2,8,8,128]{4,3,1,2,0:T(8,128)S(1)} fusion(bf16[64,16,8,128,1]{3,2,1,0,4:T(8,128)(2,1)S(1)} %copy-done.1, f32[64,8,2,8,16]{4,3,2,1,0:T(8,128)} %get-tuple-element.238, f32[64,2,8,8]{3,1,2,0:T(2,128)S(1)} %copy.112, pred[64,16]{1,0:T(8,128)(4,1)S(1)} %fusion.29), kind=kOutput, calls=%fused_computation.22 | convolution fusion | flops 34209792 | bytes 6849536 | tf_op jit(solution)/shard_map/psgjt,ptgd->psgjd/dot_general | solution.py:68
  88.0 0.6 copy.115
  88.6 3.8 %fusion.3 = f32[9,16384]{1,0:T(8,128)S(1)} fusion(f32[8,8,128,128]{3,2,1,0:T(8,128)S(1)} %bitcast.149, s32[64]{0:T(128)S(1)} %get-tuple-element.214), kind=kOutput, calls=%fused_computation.12 | convolution fusion | flops 113246784 | bytes 4784384 | tf_op jit(solution)/shard_map/dot_general | solution.py:76
  92.7 0.6 collective-permute-start.4
  93.3 3.6 %collective-permute-done.4 = f32[1,2,64,128]{3,2,1,0:T(8,128)S(1)} collective-permute-done((f32[1,2,64,128]{3,2,1,0:T(8,128)S(1)}, f32[1,2,64,128]{3,2,1,0:T(8,128)S(1)}, u32[]{:S(2)}, u32[]{:S(2)}) %collective-permute-start.4) | collective-permute-done | bytes 65568 | tf_op jit(solution)/shard_map/ppermute | solution.py:16
  96.9 1.2 fusion.19
  98.4 20.6 %all-gather.5 = bf16[1,8,2,1024]{1,2,0,3:T(2,128)(2,1)S(1)} all-gather(bf16[1,8,2,64]{1,2,0,3:T(2,128)(2,1)S(1)} %copy.125), channel_id=7, replica_groups=mesh['group'=2,'tp'=16] {'tp'}, dimensions={3}, use_global_device_ids=true | all-gather | bytes 34816 | tf_op jit(solution)/shard_map/all_gather | solution.py:127
  119.0 0.3 copy.127
  119.3 22.3 %all-gather.4 = bf16[1,8,2,1024]{1,2,0,3:T(2,128)(2,1)S(1)} all-gather(bf16[1,8,2,64]{1,2,0,3:T(2,128)(2,1)S(1)} %copy.117), channel_id=6, replica_groups=mesh['group'=2,'tp'=16] {'tp'}, dimensions={3}, use_global_device_ids=true | all-gather | bytes 34816 | tf_op jit(solution)/shard_map/all_gather | solution.py:126
  141.6 0.3 copy.119
  141.9 0.7 gather_fusion.3
  142.6 0.7 gather_fusion.2
  143.5 1.1 fusion.54
  144.7 0.9 fusion.30
  145.8 2.4 %fusion.24 = f32[8,64,128,2]{2,3,1,0:T(2,128)S(1)} fusion(bf16[8,2,64,128]{3,0,1,2:T(8,128)(2,1)S(1)} %get-tuple-element.234, f32[8,2,64,2]{1,3,2,0:T(2,128)S(1)} %get-tuple-element.236, pred[2,2]{0,1:T(4,128)(4,1)S(1)} %iota_compare_fusion.4, f32[8,2,64]{1,2,0:T(8,128)S(1)} %get-tuple-element.235), kind=kOutput, calls=%fused_computation.50 | convolution fusion | flops 3149824 | bytes 798724 | tf_op jit(solution)/shard_map/rshu,ruhd->rshd/dot_general | solution.py:106
  148.2 18.7 %all-gather.2 = f32[128,2,64]{2,1,0:T(2,128)S(1)} all-gather(f32[8,2,64]{2,1,0:T(2,128)S(1)} %get-tuple-element.209), channel_id=4, replica_groups=mesh['group'=2,'tp'=16] {'tp'}, dimensions={0}, use_global_device_ids=true | all-gather | bytes 69632 | tf_op jit(solution)/shard_map/all_gather | solution.py:20
  166.8 19.0 %all-gather.1 = f32[128,2,64]{2,1,0:T(2,128)S(1)} all-gather(f32[8,2,64]{2,1,0:T(2,128)S(1)} %get-tuple-element.212), channel_id=3, replica_groups=mesh['group'=2,'tp'=16] {'tp'}, dimensions={0}, use_global_device_ids=true | all-gather | bytes 69632 | tf_op jit(solution)/shard_map/all_gather | solution.py:20
  185.8 1.1 slice.104
  186.9 24.2 %while.19 = (s32[]{:T(128)}, f32[8,2,64]{2,1,0:T(2,128)S(1)}, f32[8,2,64]{2,1,0:T(2,128)S(1)}, f32[8,2,64,128]{3,2,1,0:T(8,128)S(1)}, f32[16,8,2,64]{3,2,1,0:T(2...) while((s32[]{:T(128)}, f32[8,2,64]{2,1,0:T(2,128)S(1)}, ...), condition=%wide.region_8.10_spmd, body=%wide.region_7.9_spmd.sunk | while | flops 399365 | bytes 1613967 | solution.py:25
  187.0 1.5 fusion.60
  188.6 1.5 fusion.60
  190.2 1.5 fusion.60
  191.8 1.5 fusion.60
  193.4 1.5 fusion.60
  195.0 1.5 fusion.60
  196.6 1.5 fusion.60
  198.2 1.5 fusion.60
  199.9 1.5 fusion.60
  201.5 1.5 fusion.60
  203.1 1.5 fusion.60
  204.7 1.5 fusion.60
  206.3 1.5 fusion.60
  207.9 1.5 fusion.60
  209.5 1.5 fusion.60
  211.1 0.5 fusion.18
  211.6 4.6 %convolution_convert_fusion = bf16[16,512]{1,0:T(8,128)(2,1)S(1)} fusion(bf16[8192,512]{1,0:T(8,128)(2,1)} %param.23, bf16[2,8,64,128]{3,2,1,0:T(8,128)(2,1)S(1)} %bitcast.154), kind=kOutput, calls=%fused_computation.33 | convolution fusion | flops 134225920 | bytes 8667136 | tf_op jit(solution)/shard_map/dot_general | solution.py:193
  216.2 0.6 reshape.265
  (72 shorter events, 3.2 us)
Async XLA Ops:
  6.5 179.3 %all-gather.8.cloned.1.call-start = ((), (), s32[]{:S(2)}) async-start(), calls=%async_computation | async-start | bytes 8912896 | tf_op jit(solution)/shard_map/all_gather | solution.py:20
  6.5 45.5 %collective-permute-start = (s32[8]{0:T(128)}, s32[8]{0:T(128)S(1)}, u32[]{:S(2)}, u32[]{:S(2)}) collective-permute-start(s32[8]{0:T(128)} %bitcast.168), channel_id=1, source_target_pairs={{0,16},{16,0},{1,17},{17,1},{2,18},{18,2},{3,19},{19,3},{4,20},{20... | collective-permute-start | bytes 104 | tf_op jit(solution)/shard_map/ppermute | solution.py:16
  45.9 3.9 %copy-start = (bf16[1,64,16,1024]{3,2,1,0:T(8,128)(2,1)S(1)}, bf16[1,64,16,1024]{3,2,1,0:T(8,128)(2,1)}, u32[]{:S(2)}) copy-start(bf16[1,64,16,1024]{3,2,1,0:T(8,128)(2,1)} %param.19) | copy-start | bytes 6291460
  49.8 2.1 copy-start.4
  55.4 4.0 %collective-permute-start.1 = (bf16[1,2,8192]{2,1,0:T(2,128)(2,1)S(1)}, bf16[1,2,8192]{2,1,0:T(2,128)(2,1)S(1)}, u32[]{:S(2)}, u32[]{:S(2)}) collective-permute-start(bf16[1,2,8192]{2,1,0:T(2,128)(2,1)S(1)} %copy.193), channel_id=1, source_target_pairs={{0,16},{16,0},{1,17},{17,1},{2,18},{18,2},{3,19},{19,3},{4,20},{20... | collective-permute-start | bytes 98312 | tf_op jit(solution)/shard_map/ppermute | solution.py:16
  74.5 9.3 %copy-start.1 = (bf16[64,16,8,128,1]{3,2,1,0,4:T(8,128)(2,1)S(1)}, bf16[64,16,8,128,1]{3,2,1,0,4:T(8,128)(2,1)}, u32[]{:S(2)}) copy-start(bf16[64,16,8,128,1]{3,2,1,0,4:T(8,128)(2,1)} %bitcast_bitcast_fusion) | copy-start | bytes 6291460
  75.7 17.5 %collective-permute-start.2 = (f32[1,2,64]{2,1,0:T(2,128)S(1)}, f32[1,2,64]{2,1,0:T(2,128)S(1)}, u32[]{:S(2)}, u32[]{:S(2)}) collective-permute-start(f32[1,2,64]{2,1,0:T(2,128)S(1)} %slice.42), channel_id=1, source_target_pairs={{0,16},{16,0},{1,17},{17,1},{2,18},{18,2},{3,19},{19,3},{4,20},{20... | collective-permute-start | bytes 1544 | tf_op jit(solution)/shard_map/ppermute | solution.py:16
  82.3 10.9 %collective-permute-start.3 = (f32[1,2,64]{2,1,0:T(2,128)S(1)}, f32[1,2,64]{2,1,0:T(2,128)S(1)}, u32[]{:S(2)}, u32[]{:S(2)}) collective-permute-start(f32[1,2,64]{2,1,0:T(2,128)S(1)} %slice.46), channel_id=1, source_target_pairs={{0,16},{16,0},{1,17},{17,1},{2,18},{18,2},{3,19},{19,3},{4,20},{20... | collective-permute-start | bytes 1544 | tf_op jit(solution)/shard_map/ppermute | solution.py:16
  88.6 9.6 %copy-start.2 = (bf16[1,8,2,64]{3,2,1,0:T(2,128)(2,1)S(1)}, bf16[1,8,2,64]{3,2,1,0:T(2,128)(2,1)}, u32[]{:S(2)}) copy-start(bf16[1,8,2,64]{3,2,1,0:T(2,128)(2,1)} %param.16) | copy-start | bytes 6148
  88.6 9.7 %copy-start.3 = (bf16[1,8,2,64]{3,2,1,0:T(2,128)(2,1)S(1)}, bf16[1,8,2,64]{3,2,1,0:T(2,128)(2,1)}, u32[]{:S(2)}) copy-start(bf16[1,8,2,64]{3,2,1,0:T(2,128)(2,1)} %param.17) | copy-start | bytes 6148
  92.7 4.3 %collective-permute-start.4 = (f32[1,2,64,128]{3,2,1,0:T(8,128)S(1)}, f32[1,2,64,128]{3,2,1,0:T(8,128)S(1)}, u32[]{:S(2)}, u32[]{:S(2)}) collective-permute-start(f32[1,2,64,128]{3,2,1,0:T(8,128)S(1)} %bitcast.167), channel_id=1, source_target_pairs={{0,16},{16,0},{1,17},{17,1},{2,18},{18,2},{3,19},{19,3},{4,20},{20... | collective-permute-start | bytes 196616 | tf_op jit(solution)/shard_map/ppermute | solution.py:16
Sparse Core Ops, SparseCore 0:
  98.3 73.7 all-gather.7
where the time goes:
time: 225 us; the launch traced here: 224 us
  blocking collectives  103 us (46%)
  other arithmetic  48 us (21%)
  local copies, waits for them, and re-layouts  24.3 us (11%)
  matrix products  22.4 us (10%)
  between operations  13.8 us (6%)
  starting transfers between devices  6.16 us (3%)
  waiting for transfers between devices  5.69 us (3%)
    all_gather x2, blocking collectives, combined_all(): gathered = jax.tree.map(lambda a: lax.all_gather(a, axis), part)  37.6 us
    add x16, other arithmetic, merge_states(): first[2] * scale_first[..., None] + second[2] * scale_second[..., None]  24.4 us
    all_gather x1, blocking collectives, per_device(): lax.all_gather(queries[0], 'tp', axis=2, tiled=True)  22.6 us
    all_gather x1, blocking collectives, per_device(): lax.all_gather(new_keys[0], 'tp', axis=2, tiled=True)  22.3 us
    all_gather x1, blocking collectives, per_device(): lax.all_gather(new_values[0], 'tp', axis=2, tiled=True)  20.6 us
    lt x1, other arithmetic, page_states(): owner_rows < row_count  10.6 us
    gather x2, local copies, waits for them, and re-layouts, page_states(): jnp.take(query_rows, clipped, axis=0)  8.94 us
    ppermute x5, starting transfers between devices, swapped(): lax.ppermute(value, axis, [(i, i ^ 1 << distance) for i in range(lax.axis...  6.16 us
  transfers between devices with their start and end apart: 6, of which 2 were waited for; matrix products, arithmetic and copies ran while one was open for 19% of the time, Pallas kernels for 0%

commit v1 on v0

--- a/solution.py
+++ b/solution.py
@@ -122,7 +122,7 @@
     step_count = queries.shape[2]
     partner_bit = lax.axis_size("group").bit_length() - 2
     query_rows, key_rows, value_rows = (
-        lax.all_gather(queries[0], "tp", axis=2, tiled=True),
+        jnp.concatenate(lax.all_gather(queries[0], "tp"), axis=2),
         lax.all_gather(new_keys[0], "tp", axis=2, tiled=True),
         lax.all_gather(new_values[0], "tp", axis=2, tiled=True),
     )

time: 225 us -> 228 us (1.013)
  transfers between devices with their start and end apart: 6 -> 6, of which waited for: 2 -> 2; matrix products, arithmetic and copies ran while one was open for 19% -> 20% of each run, Pallas kernels for 0% -> 0%
where the time goes in v1:
time: 228 us; the launch traced here: 226 us
  blocking collectives  103 us (45%)
  other arithmetic  47.9 us (21%)
  local copies, waits for them, and re-layouts  25.6 us (11%)
  matrix products  23.5 us (10%)
  between operations  13.8 us (6%)
  starting transfers between devices  6.16 us (3%)
  waiting for transfers between devices  5.69 us (2%)
    all_gather x2, blocking collectives, combined_all(): gathered = jax.tree.map(lambda a: lax.all_gather(a, axis), part)  37.7 us
    add x16, other arithmetic, merge_states(): first[2] * scale_first[..., None] + second[2] * scale_second[..., None]  24.4 us
    all_gather x1, blocking collectives, per_device(): lax.all_gather(new_keys[0], 'tp', axis=2, tiled=True)  22.5 us
    all_gather x1, blocking collectives, per_device(): lax.all_gather(queries[0], 'tp')  22.3 us
    all_gather x1, blocking collectives, per_device(): lax.all_gather(new_values[0], 'tp', axis=2, tiled=True)  20.6 us
    lt x1, other arithmetic, page_states(): owner_rows < row_count  10.6 us
    gather x2, local copies, waits for them, and re-layouts, page_states(): jnp.take(query_rows, clipped, axis=0)  8.94 us
    ppermute x5, starting transfers between devices, swapped(): lax.ppermute(value, axis, [(i, i ^ 1 << distance) for i in range(lax.axis...  6.16 us
  transfers between devices with their start and end apart: 6, of which 2 were waited for; matrix products, arithmetic and copies ran while one was open for 20% of the time, Pallas kernels for 0%

profile of v1, /device:TPU:0, one launch (start us, length us, event | category | flops | bytes accessed | tf_op | source)
XLA Modules:
  0.0 226.2 jit_solution(15470466513637657264)
XLA Ops:
  6.5 3.0 %collective-permute-start = (s32[8]{0:T(128)}, s32[8]{0:T(128)S(1)}, u32[]{:S(2)}, u32[]{:S(2)}) collective-permute-start(s32[8]{0:T(128)} %bitcast.171), channel_id=1, source_target_pairs={{0,16},{16,0},{1,17},{17,1},{2,18},{18,2},{3,19},{19,3},{4,20},{20... | collective-permute-start | bytes 104 | tf_op jit(solution)/shard_map/ppermute | solution.py:16
  9.5 0.7 fusion.40
  10.2 1.6 fusion.48
  12.0 0.7 fusion.49
  12.7 10.6 %broadcast_compare_fusion = (pred[64]{0:T(512)(128)(4,1)S(1)}, s32[64]{0:T(128)S(1)}) fusion(s32[]{:T(128)} %bitcast.22, s32[]{:T(128)} %bitcast.21, s32[]{:T(128)} %bitcast.20, s32[]{:T(128)} %bitcast.19, s32[]{:T(128)} %bitcast.18, s32[]{:T(128)} %bitcast.17, s32[]{:T(128)} %bitcast.16, s32[]{:T(128)} %bitcast.15, s32[]{:T(128)} %bitcast.12, s32[]{:T(128)} %bitcast.11, ...), kind=kLoop, calls=%fused_computation.118 | loop fusion | flops 2368 | bytes 640 | tf_op jit(solution)/shard_map/lt | solution.py:56
  23.4 0.7 copy.126
  24.1 22.3 %all_gather.27 = bf16[16,8,2,512]{3,1,2,0:T(8,128)(2,1)S(1)} all-gather(bf16[1,8,2,512]{3,1,2,0:T(8,128)(2,1)S(1)} %copy.126), channel_id=1, replica_groups=mesh['group'=2,'tp'=16] {'tp'}, dimensions={0}, use_global_device_ids=true | all-gather | bytes 278528 | tf_op jit(solution)/shard_map/all_gather | solution.py:125
  46.7 2.4 %copy.175 = bf16[128,8,8,128]{3,2,1,0:T(8,128)(2,1)S(1)} copy(bf16[128,8,8,128]{3,1,2,0:T(8,128)(2,1)} %bitcast.158) | data formatting | bytes 4194304
  49.1 1.5 bitcast_bitcast_fusion.1
  50.6 0.6 copy.176
  51.2 1.5 bitcast_bitcast_fusion
  53.0 0.7 select_reduce_fusion.1
  53.7 0.6 fusion.42
  54.3 1.3 bitcast_convert_fusion.1
  55.7 1.5 fusion.35
  57.3 0.6 collective-permute-start.1
  57.9 1.3 compare_and_fusion.2
  59.2 2.1 collective-permute-done.1
  61.3 0.4 pad_maximum_fusion
  61.7 6.1 %gather_fusion = bf16[64,2,8192]{2,1,0:T(2,128)(2,1)S(1)} fusion(bf16[9,2,8192]{2,1,0:T(2,128)(2,1)S(1)} %pad_maximum_fusion, s32[1024]{0:T(1024)S(1)} %pad_clamp_fusion.1), kind=kCustom, calls=%fused_computation.2 | custom fusion | bytes 4194560 | tf_op jit(solution)/shard_map/jit(_take)/gather | solution.py:47
  67.8 2.9 %reshape.376 = bf16[64,2,8,8,128]{4,3,2,1,0:T(8,128)(2,1)} reshape(bf16[64,2,8192]{2,1,0:T(2,128)(2,1)S(1)} %gather_fusion) | data formatting | bytes 4194304 | tf_op jit(solution)/shard_map/jit(_take)/gather | solution.py:47
  70.6 5.7 %bitcast_reduce_fusion = (f32[64,2,8,8]{3,1,2,0:T(2,128)S(1)}, f32[64,8,2,8,16]{4,3,2,1,0:T(8,128)}) fusion(pred[64,16]{1,0:T(8,128)(4,1)S(1)} %fusion.26, bf16[64,16,8,128,1]{3,2,1,0,4:T(8,128)(2,1)} %bitcast_bitcast_fusion.1, bf16[64,2,8,8,128]{4,3,2,1,0:T(8,128)(2,1)} %reshape.376, pred[64]{0:T(512)(128)(4,1)S(1)} %get-tuple-element.215), kind=kOutput, calls=%fused_computation.16 | convolution fusion | flops 34988032 | bytes 4752448 | tf_op jit(solution)/shard_map/psgjd,ptgd->psgjt/dot_general | solution.py:53
  76.9 0.6 gather_fusion.1
  77.6 0.6 collective-permute-start.2
  78.3 0.4 copy.135
  78.7 4.9 %convert_reduce_fusion = f32[64,2,8,8]{3,1,2,0:T(2,128)S(1)} fusion(f32[64,2,8,8]{3,1,2,0:T(2,128)S(1)} %copy.135, f32[64,8,2,8,16]{4,3,2,1,0:T(8,128)} %get-tuple-element.238, pred[64,16]{1,0:T(8,128)(4,1)S(1)} %fusion.26), kind=kLoop, calls=%fused_computation.20 | loop fusion | flops 909312 | bytes 590848 | tf_op jit(solution)/shard_map/reduce_sum | solution.py:71
  84.2 1.5 collective-permute-start.3
  85.7 4.2 %convolution_bitcast_fusion = f32[64,2,8,8,128]{4,3,1,2,0:T(8,128)S(1)} fusion(bf16[64,16,8,128,1]{3,2,1,0,4:T(8,128)(2,1)S(1)} %copy-done.1, f32[64,8,2,8,16]{4,3,2,1,0:T(8,128)} %get-tuple-element.238, f32[64,2,8,8]{3,1,2,0:T(2,128)S(1)} %copy.135, pred[64,16]{1,0:T(8,128)(4,1)S(1)} %fusion.26), kind=kOutput, calls=%fused_computation.22 | convolution fusion | flops 34209792 | bytes 6849536 | tf_op jit(solution)/shard_map/psgjt,ptgd->psgjd/dot_general | solution.py:68
  89.8 0.6 copy.138
  90.4 3.8 %fusion.3 = f32[9,16384]{1,0:T(8,128)S(1)} fusion(f32[8,8,128,128]{3,2,1,0:T(8,128)S(1)} %bitcast.150, s32[64]{0:T(128)S(1)} %get-tuple-element.214), kind=kOutput, calls=%fused_computation.12 | convolution fusion | flops 113246784 | bytes 4784384 | tf_op jit(solution)/shard_map/dot_general | solution.py:76
  94.5 0.6 collective-permute-start.4
  95.2 3.6 %collective-permute-done.4 = f32[1,2,64,128]{3,2,1,0:T(8,128)S(1)} collective-permute-done((f32[1,2,64,128]{3,2,1,0:T(8,128)S(1)}, f32[1,2,64,128]{3,2,1,0:T(8,128)S(1)}, u32[]{:S(2)}, u32[]{:S(2)}) %collective-permute-start.4) | collective-permute-done | bytes 65568 | tf_op jit(solution)/shard_map/ppermute | solution.py:16
  98.8 1.2 fusion.18
  100.6 20.6 %all-gather.4 = bf16[1,8,2,1024]{1,2,0,3:T(2,128)(2,1)S(1)} all-gather(bf16[1,8,2,64]{1,2,0,3:T(2,128)(2,1)S(1)} %copy.150), channel_id=6, replica_groups=mesh['group'=2,'tp'=16] {'tp'}, dimensions={3}, use_global_device_ids=true | all-gather | bytes 34816 | tf_op jit(solution)/shard_map/all_gather | solution.py:127
  121.1 0.3 copy.152
  121.5 22.5 %all-gather.3 = bf16[1,8,2,1024]{1,2,0,3:T(2,128)(2,1)S(1)} all-gather(bf16[1,8,2,64]{1,2,0,3:T(2,128)(2,1)S(1)} %copy.140), channel_id=5, replica_groups=mesh['group'=2,'tp'=16] {'tp'}, dimensions={3}, use_global_device_ids=true | all-gather | bytes 34816 | tf_op jit(solution)/shard_map/all_gather | solution.py:126
  144.0 0.3 copy.142
  144.3 0.7 gather_fusion.3
  145.0 0.7 gather_fusion.2
  145.9 1.1 fusion.50
  147.1 0.9 fusion.27
  148.2 2.4 %fusion.21 = f32[8,64,128,2]{2,3,1,0:T(2,128)S(1)} fusion(bf16[8,2,64,128]{3,0,1,2:T(8,128)(2,1)S(1)} %get-tuple-element.234, f32[8,2,64,2]{1,3,2,0:T(2,128)S(1)} %get-tuple-element.236, pred[2,2]{0,1:T(4,128)(4,1)S(1)} %iota_compare_fusion.4, f32[8,2,64]{1,2,0:T(8,128)S(1)} %get-tuple-element.235), kind=kOutput, calls=%fused_computation.47 | convolution fusion | flops 3149824 | bytes 798724 | tf_op jit(solution)/shard_map/rshu,ruhd->rshd/dot_general | solution.py:106
  150.6 18.7 %all-gather.1 = f32[128,2,64]{2,1,0:T(2,128)S(1)} all-gather(f32[8,2,64]{2,1,0:T(2,128)S(1)} %get-tuple-element.209), channel_id=3, replica_groups=mesh['group'=2,'tp'=16] {'tp'}, dimensions={0}, use_global_device_ids=true | all-gather | bytes 69632 | tf_op jit(solution)/shard_map/all_gather | solution.py:20
  169.3 19.0 %all-gather = f32[128,2,64]{2,1,0:T(2,128)S(1)} all-gather(f32[8,2,64]{2,1,0:T(2,128)S(1)} %get-tuple-element.212), channel_id=2, replica_groups=mesh['group'=2,'tp'=16] {'tp'}, dimensions={0}, use_global_device_ids=true | all-gather | bytes 69632 | tf_op jit(solution)/shard_map/all_gather | solution.py:20
  188.3 1.1 slice.104
  189.4 24.1 %while.19 = (s32[]{:T(128)}, f32[8,2,64]{2,1,0:T(2,128)S(1)}, f32[8,2,64]{2,1,0:T(2,128)S(1)}, f32[8,2,64,128]{3,2,1,0:T(8,128)S(1)}, f32[16,8,2,64]{3,2,1,0:T(2...) while((s32[]{:T(128)}, f32[8,2,64]{2,1,0:T(2,128)S(1)}, ...), condition=%wide.region_8.10_spmd, body=%wide.region_7.9_spmd.sunk | while | flops 399365 | bytes 1613967 | solution.py:25
  189.5 1.5 fusion.57
  191.1 1.5 fusion.57
  192.7 1.5 fusion.57
  194.3 1.5 fusion.57
  195.9 1.5 fusion.57
  197.5 1.5 fusion.57
  199.1 1.5 fusion.57
  200.7 1.5 fusion.57
  202.4 1.5 fusion.57
  204.0 1.5 fusion.57
  205.6 1.5 fusion.57
  207.2 1.5 fusion.57
  208.8 1.5 fusion.57
  210.4 1.5 fusion.57
  212.0 1.5 fusion.57
  213.6 0.5 fusion.17
  214.1 4.6 %convolution_convert_fusion = bf16[16,512]{1,0:T(8,128)(2,1)S(1)} fusion(bf16[8192,512]{1,0:T(8,128)(2,1)} %param.23, bf16[2,8,64,128]{3,2,1,0:T(8,128)(2,1)S(1)} %bitcast.157), kind=kOutput, calls=%fused_computation.33 | convolution fusion | flops 134225920 | bytes 8667136 | tf_op jit(solution)/shard_map/dot_general | solution.py:193
  218.7 0.6 reshape.268
  (77 shorter events, 4.1 us)
Async XLA Ops:
  6.5 181.8 %all-gather.7.cloned.1.call-start = ((), (), s32[]{:S(2)}) async-start(), calls=%async_computation | async-start | bytes 8912896 | tf_op jit(solution)/shard_map/all_gather | solution.py:20
  6.5 46.2 %collective-permute-start = (s32[8]{0:T(128)}, s32[8]{0:T(128)S(1)}, u32[]{:S(2)}, u32[]{:S(2)}) collective-permute-start(s32[8]{0:T(128)} %bitcast.171), channel_id=1, source_target_pairs={{0,16},{16,0},{1,17},{17,1},{2,18},{18,2},{3,19},{19,3},{4,20},{20... | collective-permute-start | bytes 104 | tf_op jit(solution)/shard_map/ppermute | solution.py:16
  46.7 3.9 %copy-start = (bf16[1,64,16,1024]{3,2,1,0:T(8,128)(2,1)S(1)}, bf16[1,64,16,1024]{3,2,1,0:T(8,128)(2,1)}, u32[]{:S(2)}) copy-start(bf16[1,64,16,1024]{3,2,1,0:T(8,128)(2,1)} %param.19) | copy-start | bytes 6291460
  50.6 2.1 copy-start.4
  57.3 4.0 %collective-permute-start.1 = (bf16[1,2,8192]{2,1,0:T(2,128)(2,1)S(1)}, bf16[1,2,8192]{2,1,0:T(2,128)(2,1)S(1)}, u32[]{:S(2)}, u32[]{:S(2)}) collective-permute-start(bf16[1,2,8192]{2,1,0:T(2,128)(2,1)S(1)} %copy.224), channel_id=1, source_target_pairs={{0,16},{16,0},{1,17},{17,1},{2,18},{18,2},{3,19},{19,3},{4,20},{20... | collective-permute-start | bytes 98312 | tf_op jit(solution)/shard_map/ppermute | solution.py:16
  76.4 9.3 %copy-start.1 = (bf16[64,16,8,128,1]{3,2,1,0,4:T(8,128)(2,1)S(1)}, bf16[64,16,8,128,1]{3,2,1,0,4:T(8,128)(2,1)}, u32[]{:S(2)}) copy-start(bf16[64,16,8,128,1]{3,2,1,0,4:T(8,128)(2,1)} %bitcast_bitcast_fusion) | copy-start | bytes 6291460
  77.6 17.5 %collective-permute-start.2 = (f32[1,2,64]{2,1,0:T(2,128)S(1)}, f32[1,2,64]{2,1,0:T(2,128)S(1)}, u32[]{:S(2)}, u32[]{:S(2)}) collective-permute-start(f32[1,2,64]{2,1,0:T(2,128)S(1)} %slice.42), channel_id=1, source_target_pairs={{0,16},{16,0},{1,17},{17,1},{2,18},{18,2},{3,19},{19,3},{4,20},{20... | collective-permute-start | bytes 1544 | tf_op jit(solution)/shard_map/ppermute | solution.py:16
  84.2 10.9 %collective-permute-start.3 = (f32[1,2,64]{2,1,0:T(2,128)S(1)}, f32[1,2,64]{2,1,0:T(2,128)S(1)}, u32[]{:S(2)}, u32[]{:S(2)}) collective-permute-start(f32[1,2,64]{2,1,0:T(2,128)S(1)} %slice.46), channel_id=1, source_target_pairs={{0,16},{16,0},{1,17},{17,1},{2,18},{18,2},{3,19},{19,3},{4,20},{20... | collective-permute-start | bytes 1544 | tf_op jit(solution)/shard_map/ppermute | solution.py:16
  90.4 9.6 %copy-start.2 = (bf16[1,8,2,64]{3,2,1,0:T(2,128)(2,1)S(1)}, bf16[1,8,2,64]{3,2,1,0:T(2,128)(2,1)}, u32[]{:S(2)}) copy-start(bf16[1,8,2,64]{3,2,1,0:T(2,128)(2,1)} %param.16) | copy-start | bytes 6148
  90.4 9.7 %copy-start.3 = (bf16[1,8,2,64]{3,2,1,0:T(2,128)(2,1)S(1)}, bf16[1,8,2,64]{3,2,1,0:T(2,128)(2,1)}, u32[]{:S(2)}) copy-start(bf16[1,8,2,64]{3,2,1,0:T(2,128)(2,1)} %param.17) | copy-start | bytes 6148
  94.5 4.3 %collective-permute-start.4 = (f32[1,2,64,128]{3,2,1,0:T(8,128)S(1)}, f32[1,2,64,128]{3,2,1,0:T(8,128)S(1)}, u32[]{:S(2)}, u32[]{:S(2)}) collective-permute-start(f32[1,2,64,128]{3,2,1,0:T(8,128)S(1)} %bitcast.170), channel_id=1, source_target_pairs={{0,16},{16,0},{1,17},{17,1},{2,18},{18,2},{3,19},{19,3},{4,20},{20... | collective-permute-start | bytes 196616 | tf_op jit(solution)/shard_map/ppermute | solution.py:16
Sparse Core Ops, SparseCore 0:
  100.1 73.8 all-gather.6
